TPU v7x, 256 devices: a whole 4x4x8 slice. The times are simulated.
256 devices in a mesh: seq: 32 (over y, z), head: 8 (over x, core).
Axes of the slice: x: 4, y: 4, z: 8, core: 2. Of those that a mesh axis runs over, the one named last changes fastest.
Arguments:
- tokens: bfloat16 [12288, 4096], P('seq', 'head'), may hold values from -6 to 6
- norm_gain: float32 [4096], replicated, may hold values from 0.25 to 1.75
- w_in: bfloat16 [4096, 8, 2304], P('seq', 'head'), may hold values from -0.09375 to 0.09375
- w_dt: bfloat16 [4096, 128], P('seq', 'head'), may hold values from -0.09375 to 0.09375
- dt_bias: float32 [128], P('head'), may hold values from -3 to -1
- a_log: float32 [128], P('head'), may hold values from -11 to -1
- d_skip: float32 [128], P('head'), may hold values from 0.5 to 1.5
- conv_w: float32 [4, 8, 1280], P(None, 'head'), may hold values from -0.5 to 0.5
- conv_b: float32 [8, 1280], P('head'), may hold values from -0.5 to 0.5
- gate_gain: float32 [8, 1024], P('head'), may hold values from 0.25 to 1.75
- w_out: bfloat16 [8, 1024, 4096], P('head'), may hold values from -0.09375 to 0.09375
Outputs:
- mixed: bfloat16 [12288, 4096], P('seq', 'head')
All inputs are finite; a program needn't handle non-finite values.
Results may differ from a plain program's by a relative error of at most 0.018.
Values may be sent and summed in bfloat16 or wider, within the bound.
A program may use at most 128 MiB of HBM per device.

v0:
```python
from functools import partial
import jax
import jax.numpy as jnp
from jax import lax
from jax.sharding import Mesh
from jax.sharding import PartitionSpec as P

STRETCH = 128
SEQ = ("seq_0", "seq_1")
EPS = 1e-05
HIGHEST = lax.Precision.HIGHEST


def from_behind(shard, axis, by):
    count = lax.axis_size(axis)
    pairs = [(i, i + by) for i in range(count) if 0 <= i + by < count]
    return lax.ppermute(shard, axis, pairs)


def sent_together(arrays, axis, dim, along):
    both = jnp.concatenate(arrays, axis=along)
    result, at, gathered = (lax.all_gather(both, axis, axis=dim, tiled=True), 0, [])
    for a in arrays:
        gathered.append(lax.slice_in_dim(result, at, at + a.shape[along], axis=along))
        at += a.shape[along]
    return tuple(gathered)


def neutral_like(shard, identity):
    return jax.tree.map(
        lambda part, zero: jnp.zeros_like(part) + jnp.asarray(zero, part.dtype), shard, identity
    )


def entering(shard, axes, combine, identity):
    before = start = neutral_like(shard, identity)
    running = shard
    for axis in reversed(axes):
        count, index = (lax.axis_size(axis), lax.axis_index(axis))
        pieces = jax.tree.map(
            lambda part, kind: lax.all_gather(part.astype(kind), axis),
            running,
            (jnp.bfloat16, jnp.bfloat16),
        )
        inside, running = (start, start)
        for k in range(count):
            passed = k < index
            running = combine(
                running, jax.tree.map(lambda part, own: part[k].astype(own.dtype), pieces, shard)
            )
            inside = jax.tree.map(lambda new, old: jnp.where(passed, new, old), running, inside)
        before = combine(inside, before)
    return before


def normalize(values, gain):
    squares = jnp.mean(values * values, axis=-1, keepdims=True)
    return values * lax.rsqrt(squares + EPS) * gain


def state_block(inputs, step_size, log_decay, in_map, out_map, block_len):
    length = inputs.shape[0]
    stretch_count = length // block_len
    head_count = inputs.shape[1]
    head_size = inputs.shape[2]
    state_size = in_map.shape[1]
    shaped = (
        inputs.reshape(stretch_count, block_len, head_count, head_size),
        step_size.reshape(stretch_count, block_len, head_count),
        log_decay.reshape(stretch_count, block_len, head_count),
        in_map.reshape(stretch_count, block_len, state_size),
        out_map.reshape(stretch_count, block_len, state_size),
    )
    causal = jnp.arange(block_len)[:, None] >= jnp.arange(block_len)[None, :]

    def advance(state_now, pieces):
        stretch_in, stretch_step, stretch_log, stretch_b, stretch_c = pieces
        cumulative = jnp.cumsum(stretch_log, axis=0)
        gap_log = cumulative[:, None, :] - cumulative[None, :, :]
        decays = jnp.where(
            causal[:, :, None], jnp.exp(jnp.where(causal[:, :, None], gap_log, 0.0)), 0.0
        )
        scores = jnp.dot(stretch_c, stretch_b.T, preferred_element_type=jnp.float32)
        wide_c = stretch_c.astype(jnp.float32)
        wide_b = stretch_b.astype(jnp.float32)
        weights = scores[:, :, None] * decays * stretch_step[None, :, :]
        within = jnp.einsum("ijh,jhp->ihp", weights, stretch_in, precision=HIGHEST)
        across = jnp.exp(cumulative)[:, :, None] * jnp.einsum(
            "in,hpn->ihp", wide_c, state_now, precision=HIGHEST
        )
        to_end = jnp.exp(cumulative[-1][None, :] - cumulative) * stretch_step
        fresh_state = jnp.einsum("jh,jhp,jn->hpn", to_end, stretch_in, wide_b, precision=HIGHEST)
        state_next = jnp.exp(cumulative[-1])[:, None, None] * state_now + fresh_state
        return (state_next, within + across)

    start_state = jnp.zeros((head_count, head_size, state_size), jnp.float32)
    final, outputs = lax.scan(advance, start_state, shaped)
    return (outputs.reshape(length, head_count, head_size), final)


def link_states(earlier, later):
    return (earlier[0] + later[0], jnp.exp(later[0])[:, :, None, None] * earlier[1] + later[1])


def body(tokens, norm_gain, w_in, w_dt, dt_bias, a_log, d_skip, conv_w, conv_b, gate_gain, w_out):
    local_rows = tokens.shape[0]
    kernel_len = conv_w.shape[0]
    groups, group_width = gate_gain.shape
    head_count = dt_bias.shape[0]
    per_group = head_count // groups
    head_size = group_width // per_group
    state_size = (conv_b.shape[1] - group_width) // 2
    gathered = lax.all_gather(tokens, "head", axis=1, tiled=True)
    normed = normalize(gathered.astype(jnp.float32), norm_gain).astype(jnp.bfloat16)
    before = from_behind(normed[local_rows - kernel_len + 1 :], SEQ, 1)
    source = jnp.concatenate([before, normed], axis=0)
    span_rows = source.shape[0]
    flat_in = w_in.reshape(w_in.shape[0], groups * w_in.shape[2])
    pieces = sent_together((flat_in, w_dt), SEQ, 0, 1)
    proj_sum = jnp.dot(source, pieces[0], preferred_element_type=jnp.float32)
    step_sum = jnp.dot(source, pieces[1], preferred_element_type=jnp.float32)
    projected = proj_sum.astype(jnp.bfloat16).reshape(span_rows, groups, w_in.shape[2])
    step_size = jax.nn.softplus(step_sum[span_rows - local_rows :] + dt_bias[None, :])
    gate_raw = projected[span_rows - local_rows :, :, :group_width]
    extended = projected[:, :, group_width:]
    summed = conv_b[None, :, :]
    for offset in range(kernel_len):
        summed = summed + conv_w[offset][None, :, :] * extended[
            offset : offset + local_rows
        ].astype(jnp.float32)
    narrow = lax.optimization_barrier(jax.nn.silu(summed).astype(jnp.bfloat16))
    convolved = narrow.astype(jnp.float32)
    inputs = convolved[:, :, :group_width].reshape(local_rows, groups, per_group, head_size)
    in_map = narrow[:, :, group_width : group_width + state_size]
    out_map = narrow[:, :, group_width + state_size :]
    step_grouped = step_size.reshape(local_rows, groups, per_group)
    log_decay = -jnp.exp(a_log).reshape(groups, per_group)[None, :, :] * step_grouped
    run_block = jax.vmap(
        partial(state_block, block_len=STRETCH), in_axes=(1, 1, 1, 1, 1), out_axes=(1, 0)
    )
    local_out, ending = run_block(inputs, step_grouped, log_decay, in_map, out_map)
    totals = jnp.sum(log_decay, axis=0)
    identity = (jnp.zeros_like(totals), jnp.zeros_like(ending))
    prior_decay, incoming = entering((totals, ending), SEQ, link_states, identity)
    cumulative = jnp.exp(jnp.cumsum(log_decay, axis=0))
    carried = (
        jnp.einsum("tgn,ghpn->tghp", out_map.astype(jnp.float32), incoming, precision=HIGHEST)
        * cumulative[:, :, :, None]
    )
    outputs = local_out + carried + d_skip.reshape(groups, per_group)[None, :, :, None] * inputs
    gated = outputs.reshape(local_rows, groups, group_width) * jax.nn.silu(
        gate_raw.astype(jnp.float32)
    )
    normed_out = normalize(gated, gate_gain[None, :, :]).astype(jnp.bfloat16)
    flat_out = normed_out.reshape(local_rows, groups * group_width)
    terms = jnp.dot(
        flat_out,
        w_out.reshape(groups * group_width, w_out.shape[2]),
        preferred_element_type=jnp.float32,
    )
    return lax.psum_scatter(terms.astype(jnp.bfloat16), "head", scatter_dimension=1, tiled=True)


def solution(mesh):
    split = Mesh(mesh.devices.reshape(4, 8, mesh.shape["head"]), ("seq_0", "seq_1", "head"))
    in_specs = (
        P(SEQ, "head"),
        P(),
        P(SEQ, "head", None),
        P(SEQ, "head"),
        P("head"),
        P("head"),
        P("head"),
        P(None, "head", None),
        P("head", None),
        P("head", None),
        P("head", None, None),
    )
    out_specs = P(SEQ, "head")
    return jax.shard_map(body, mesh=split, in_specs=in_specs, out_specs=out_specs, check_vma=False)
```

profile of v0, /device:TPU:8, one launch (start us, length us, event | category | flops | bytes accessed | tf_op | source)
XLA Modules:
  0.0 413.0 jit_solution(1749421173129096668)
XLA Ops:
  10.2 32.1 %all-gather.7.cloned.1.call-done = bf16[384,4096]{1,0:T(8,128)(2,1)} async-done(((bf16[384,512]{1,0:T(8,128)(2,1)}), bf16[384,4096]{1,0:T(8,128)(2,1)}) %all-gather.7.cloned.1.call-update) | async-done | bytes 3145744 | tf_op jit(solution)/shard_map/all_gather | solution.py:113
  42.3 2.7 fusion.45
  46.3 3.5 collective-permute-start
  49.9 4.3 %collective-permute-done = bf16[3,4096]{1,0:T(4,128)(2,1)S(1)} collective-permute-done((bf16[3,4096]{1,0:T(4,128)(2,1)S(1)}, bf16[3,4096]{1,0:T(4,128)(2,1)S(1)}, u32[]{:S(2)}, u32[]{:S(2)}) %collective-permute-start) | collective-permute-done | bytes 24608 | tf_op jit(solution)/shard_map/ppermute | solution.py:17
  54.2 145.0 %all-gather.9.cloned.1.call-done = bf16[4096,2320]{1,0:T(8,128)(2,1)} async-done(((bf16[128,2320]{1,0:T(8,128)(2,1)}), bf16[4096,2320]{1,0:T(8,128)(2,1)}) %all-gather.9.cloned.1.call-update) | async-done | bytes 19005456 | tf_op jit(solution)/shard_map/all_gather | solution.py:22
  199.2 13.4 %fusion.54 = bf16[387,1,2304]{2,0,1:T(8,128)(2,1)S(1)} fusion(bf16[4096,2320]{1,0:T(8,128)(2,1)} %all-gather.9.cloned.1.call-done, bf16[384,4096]{1,0:T(8,128)(2,1)} %copy-done.4, bf16[3,4096]{1,0:T(4,128)(2,1)S(1)} %collective-permute-done), kind=kOutput, calls=%fused_computation.61 | convolution fusion | flops 7311612928 | bytes 23827968 | tf_op jit(solution)/shard_map/dot_general | solution.py:120
  215.5 2.3 fusion.162
  220.2 3.2 copy.55
  223.4 59.6 %while.14 = (s32[]{:T(128)}, f32[1,16,64,128]{3,2,1,0:T(8,128)S(1)}, f32[3,1,128,16,64]{2,0,4,3,1:T(4,128)}, f32[3,1,128,16]{3,2,1,0:T(8,128)S(1)}, f32[3,1,128,...) while((s32[]{:T(128)}, ...), condition=%wide.region_3.4_spmd.clone.clone, body=%wide.region_1.3_spmd.clone.clone.sunk | while | flops 610682880 | bytes 5721559 | solution.py:97
  224.5 3.3 fusion.191
  229.4 13.8 %dynamic_update_slice.7 = f32[3,1,128,16,64]{2,0,4,3,1:T(4,128)} dynamic-update-slice(f32[3,1,128,16,64]{2,0,4,3,1:T(4,128)} %get-tuple-element.246, f32[1,1,128,16,64]{2,0,4,3,1:T(1,128)S(1)} %bitcast.242, s32[]{:T(128)S(6)} %copy.92, s32[]{:T(128)} %constant.25.clone.1..sunk, s32[]{:T(128)} %constant.25.clone.1..sunk, s32[]{:T(128)} %constant.25.clone.1..sunk, s32[]{:T(128)} %constant.25.clone.1..sunk) | dynamic-update-slice | bytes 1048580 | tf_op jit(solution)/shard_map/vmap()/while/body/jit(dynamic_update_index_in_dim)/dynamic_update_slice | solution.py:97
  244.4 3.3 fusion.191
  249.3 13.8 %dynamic_update_slice.7 = f32[3,1,128,16,64]{2,0,4,3,1:T(4,128)} dynamic-update-slice(f32[3,1,128,16,64]{2,0,4,3,1:T(4,128)} %get-tuple-element.246, f32[1,1,128,16,64]{2,0,4,3,1:T(1,128)S(1)} %bitcast.242, s32[]{:T(128)S(6)} %copy.92, s32[]{:T(128)} %constant.25.clone.1..sunk, s32[]{:T(128)} %constant.25.clone.1..sunk, s32[]{:T(128)} %constant.25.clone.1..sunk, s32[]{:T(128)} %constant.25.clone.1..sunk) | dynamic-update-slice | bytes 1048580 | tf_op jit(solution)/shard_map/vmap()/while/body/jit(dynamic_update_index_in_dim)/dynamic_update_slice | solution.py:97
  264.3 3.3 fusion.191
  269.2 13.8 %dynamic_update_slice.7 = f32[3,1,128,16,64]{2,0,4,3,1:T(4,128)} dynamic-update-slice(f32[3,1,128,16,64]{2,0,4,3,1:T(4,128)} %get-tuple-element.246, f32[1,1,128,16,64]{2,0,4,3,1:T(1,128)S(1)} %bitcast.242, s32[]{:T(128)S(6)} %copy.92, s32[]{:T(128)} %constant.25.clone.1..sunk, s32[]{:T(128)} %constant.25.clone.1..sunk, s32[]{:T(128)} %constant.25.clone.1..sunk, s32[]{:T(128)} %constant.25.clone.1..sunk) | dynamic-update-slice | bytes 1048580 | tf_op jit(solution)/shard_map/vmap()/while/body/jit(dynamic_update_index_in_dim)/dynamic_update_slice | solution.py:97
  285.4 15.7 %all-reduce = bf16[128]{0:T(256)(128)(2,1)S(1)} all-reduce(bf16[128]{0:T(256)(128)(2,1)S(1)} %dynamic-update-slice), channel_id=2, replica_groups=mesh['seq_0'=4,'seq_1'=8,'head'=8] {'seq_1'}, use_global_device_ids=true, to_apply=%add | all-reduce | flops 128 | bytes 512
  301.3 21.9 %all-gather.13.cloned.1.call-done = bf16[8,16,64,128]{3,2,1,0:T(8,128)(2,1)} async-done(((bf16[1,16,64,128]{3,2,1,0:T(8,128)(2,1)}), bf16[8,16,64,128]{3,2,1,0:T(8,128)(2,1)}) %all-gather.13.cloned.1.call-update) | async-done | bytes 2097168 | tf_op jit(solution)/shard_map/all_gather | solution.py:41
  323.1 2.8 fusion.106
  326.0 8.1 %all_gather.27 = bf16[4,1,16]{2,1,0:T(2,128)(2,1)S(1)} all-gather(bf16[1,1,16]{2,1,0:T(2,128)(2,1)S(1)} %get-tuple-element.156), channel_id=1, replica_groups=mesh['seq_0'=4,'seq_1'=8,'head'=8] {'seq_0'}, dimensions={0}, use_global_device_ids=true | all-gather | bytes 160 | tf_op jit(solution)/shard_map/all_gather | solution.py:41
  335.8 2.8 transpose.64
  338.7 11.5 %all-gather.11.cloned.1.call-done = bf16[4,1,16,64,128]{4,3,2,1,0:T(8,128)(2,1)} async-done(((bf16[1,1,16,64,128]{4,3,2,1,0:T(8,128)(2,1)}), bf16[4,1,16,64,128]{4,3,2,1,0:T(8,128)(2,1)}) %all-gather.11.cloned.1.call-update) | async-done | bytes 1048592 | tf_op jit(solution)/shard_map/all_gather | solution.py:41
  350.2 4.7 %fusion.69 = f32[384,1,16,64]{0,3,2,1:T(8,128)} fusion(f32[384,1,16,64]{0,3,2,1:T(8,128)S(1)} %transpose.64, f32[384,1,16,64]{0,3,2,1:T(8,128)S(1)} %bitcast.245, f32[16]{0:T(128)S(1)} %copy-done.12, f32[384,16]{0,1:T(8,128)S(1)} %fusion.139, bf16[4,1,16,64,128]{4,3,2,1,0:T(8,128)(2,1)} %all-gather.11.cloned.1.call-done, f32[16]{0:T(128)S(1)} %get-tuple-element.173, ...), kind=kOutput, calls=%fused_computation.78 | convolution fusion | flops 611844096 | bytes 7988108 | tf_op jit(solution)/shard_map/tgn,ghpn->tghp/dot_general | solution.py:147
  357.6 8.7 %fusion.48 = bf16[384,4096]{1,0:T(8,128)(2,1)} fusion(bf16[1,1024,4096]{2,1,0:T(8,128)(2,1)} %param.23, f32[1024]{0:T(1024)S(1)} %bitcast.251, f32[384]{0:T(512)S(1)} %add_rsqrt_fusion, f32[384,1,1024]{2,0,1:T(8,128)S(1)} %copy.63, bf16[387,1,2304]{2,0,1:T(8,128)(2,1)S(1)} %copy-done.2), kind=kOutput, calls=%fused_computation.59 | convolution fusion | flops 3226337280 | bytes 13899776 | tf_op jit(solution)/shard_map/dot_general | solution.py:156
  366.4 40.1 %reduce-scatter.2.cloned.1.call-done = bf16[384,512]{1,0:T(8,128)(2,1)} async-done(((bf16[384,4096]{1,0:T(8,128)(2,1)}), bf16[384,512]{1,0:T(8,128)(2,1)}) %reduce-scatter.2.cloned.1.call-update) | async-done | bytes 393232 | tf_op jit(solution)/shard_map/reduce_scatter | solution.py:161
  (114 shorter events, 24.6 us)
Async XLA Ops:
  6.5 3.6 copy-start.10
  6.5 35.8 %all-gather.7.cloned.1.call-start = ((), (), s32[]{:S(2)}) async-start(), calls=%async_computation.1 | async-start | bytes 3538944 | tf_op jit(solution)/shard_map/all_gather | solution.py:113
  7.3 191.9 %all-gather.9.cloned.1.call-start = ((), (), s32[]{:S(2)}) async-start(), calls=%async_computation.2 | async-start | bytes 20545536 | tf_op jit(solution)/shard_map/all_gather | solution.py:22
  10.1 34.9 %copy-start.7 = (f32[4096]{0:T(1024)S(1)}, f32[4096]{0:T(1024)}, u32[]{:S(2)}) copy-start(f32[4096]{0:T(1024)} %param.14) | copy-start | bytes 49156
  10.1 313.0 %all-gather.13.cloned.1.call-start = ((), (), s32[]{:S(2)}) async-start(), calls=%async_computation.5 | async-start | bytes 2359296 | tf_op jit(solution)/shard_map/all_gather | solution.py:41
  42.3 2.8 copy-start
  45.1 4.6 %copy-start.6 = (f32[4,1,1280]{2,1,0:T(1,128)S(1)}, f32[4,1,1280]{2,1,0:T(1,128)}, u32[]{:S(2)}) copy-start(f32[4,1,1280]{2,1,0:T(1,128)} %param.20) | copy-start | bytes 61444
  45.1 4.7 %copy-start.8 = (f32[1,1280]{1,0:T(1,128)S(1)}, f32[1,1280]{1,0:T(1,128)}, u32[]{:S(2)}) copy-start(f32[1,1280]{1,0:T(1,128)} %param.21) | copy-start | bytes 15364
  46.2 3.5 copy-start.4
  46.3 7.9 %collective-permute-start = (bf16[3,4096]{1,0:T(4,128)(2,1)S(1)}, bf16[3,4096]{1,0:T(4,128)(2,1)S(1)}, u32[]{:S(2)}, u32[]{:S(2)}) collective-permute-start(bf16[3,4096]{1,0:T(4,128)(2,1)S(1)} %slice.201), channel_id=1, source_target_pairs={{0,8},{8,16},{16,24},{24,32},{32,40},{40,48},{48,56},{56,64},{64,7... | collective-permute-start | bytes 73736 | tf_op jit(solution)/shard_map/ppermute | solution.py:17
  212.6 1.3 copy-start.1
  212.6 2.9 copy-start.5
  213.9 3.9 copy-start.3
  213.9 1.5 copy-start.11
  223.4 60.5 %copy-start.13 = (u32[256]{0:T(256)S(1)}, u32[256]{0:T(256)}, u32[]{:S(2)}) copy-start(u32[256]{0:T(256)} %constant.77) | copy-start | bytes 3076
  283.8 66.4 %all-gather.11.cloned.1.call-start = ((), (), s32[]{:S(2)}) async-start(), calls=%async_computation.3 | async-start | bytes 1310720 | tf_op jit(solution)/shard_map/all_gather | solution.py:41
  325.9 80.6 %reduce-scatter.2.cloned.1.call-start = ((), (), s32[]{:S(2)}) async-start(), calls=%async_computation.4 | async-start | bytes 3538944 | tf_op jit(solution)/shard_map/reduce_scatter | solution.py:161
  335.4 14.7 %copy-start.12 = (f32[16]{0:T(128)S(1)}, f32[16]{0:T(128)}, u32[]{:S(2)}) copy-start(f32[16]{0:T(128)} %param.19) | copy-start | bytes 196
  354.9 2.0 copy-start.2
  356.9 0.7 copy-start.9
Sparse Core Ops, SparseCore 0:
  9.2 33.0 all-gather.6
  44.9 154.2 all-gather.8
  283.9 39.1 all-gather.12
  326.1 24.0 all-gather.10
  366.5 39.9 reduce-scatter.1
where the time goes:
time: 415 us; the launch traced here: 413 us
  waiting for transfers between devices  256 us (62%)
  local copies, waits for them, and re-layouts  56.8 us (14%)
  matrix products  45.5 us (11%)
  blocking collectives  23.8 us (6%)
  between operations  14.1 us (3%)
  other arithmetic  13.3 us (3%)
    all_gather x1, waiting for transfers between devices, sent_together(): lax.all_gather(both, axis, axis=dim, tiled=True)  145 us
    dynamic_update_slice x3, local copies, waits for them, and re-layouts, state_block(): final, outputs = lax.scan(advance, start_state, shaped)  41.5 us
    reduce_scatter x1, waiting for transfers between devices, body(): lax.psum_scatter(terms.astype(jnp.bfloat16), 'head', scatter_dimension=1,...  40.1 us
    all_gather x2, waiting for transfers between devices, entering(): lax.all_gather(part.astype(kind), axis)  33.4 us
    all_gather x1, waiting for transfers between devices, body(): gathered = lax.all_gather(tokens, 'head', axis=1, tiled=True)  32.1 us
    unnamed x1, blocking collectives  15.7 us
    dot_general x1, matrix products, body(): proj_sum = jnp.dot(source, pieces[0], preferred_element_type=jnp.float32)  13.4 us
    dot_general x3, matrix products, advance(): within = jnp.einsum('ijh,jhp->ihp', weights, stretch_in, precision=HIGHEST)  9.81 us
  transfers between devices with their start and end apart: 6, of which 6 were waited for; matrix products, arithmetic and copies ran while one was open for 3% of the time, Pallas kernels for 0%

commit v1 on v0

--- a/solution.py
+++ b/solution.py
@@ -110,7 +110,8 @@
     per_group = head_count // groups
     head_size = group_width // per_group
     state_size = (conv_b.shape[1] - group_width) // 2
-    gathered = lax.all_gather(tokens, "head", axis=1, tiled=True)
+    copies = jnp.concatenate([tokens] * lax.axis_size("head"), axis=1)
+    gathered = lax.all_to_all(copies, "head", 1, 1, tiled=True)
     normed = normalize(gathered.astype(jnp.float32), norm_gain).astype(jnp.bfloat16)
     before = from_behind(normed[local_rows - kernel_len + 1 :], SEQ, 1)
     source = jnp.concatenate([before, normed], axis=0)

time: 415 us -> 390 us (0.940)
  waiting for transfers between devices: 256 us -> 209 us
  local copies, waits for them, and re-layouts: 56.8 us -> 70.5 us
  starting transfers between devices: 3.63 us -> 8.92 us
    all_gather x1, waiting for transfers between devices: 145 us -> 91.9 us  [sent_together(): lax.all_gather(both, axis, axis=dim, tiled=True)]
    all_to_all x0 -> x1, waiting for transfers between devices: none -> 38.3 us  [body(): gathered = lax.all_to_all(copies, 'head', 1, 1, tiled=True)]
    all_gather x1 -> x0, waiting for transfers between devices: 32.1 us -> none  [body(): gathered = lax.all_gather(tokens, 'head', axis=1, tiled=True)]
    all_to_all x0 -> x2, local copies, waits for them, and re-layouts: none -> 6.41 us  [body(): gathered = lax.all_to_all(copies, 'head', 1, 1, tiled=True)]
    all_to_all x0 -> x1, starting transfers between devices: none -> 4.57 us  [body(): gathered = lax.all_to_all(copies, 'head', 1, 1, tiled=True)]
  transfers between devices with their start and end apart: 6 -> 6, of which waited for: 6 -> 6; matrix products, arithmetic and copies ran while one was open for 3% -> 5% of each run, Pallas kernels for 0% -> 0%
where the time goes in v1:
time: 390 us; the launch traced here: 388 us
  waiting for transfers between devices  209 us (54%)
  local copies, waits for them, and re-layouts  70.5 us (18%)
  matrix products  47.3 us (12%)
  blocking collectives  23.5 us (6%)
  other arithmetic  14.8 us (4%)
  between operations  14.1 us (4%)
  starting transfers between devices  8.92 us (2%)
    all_gather x1, waiting for transfers between devices, sent_together(): lax.all_gather(both, axis, axis=dim, tiled=True)  91.9 us
    dynamic_update_slice x3, local copies, waits for them, and re-layouts, state_block(): final, outputs = lax.scan(advance, start_state, shaped)  41.5 us
    reduce_scatter x1, waiting for transfers between devices, body(): lax.psum_scatter(terms.astype(jnp.bfloat16), 'head', scatter_dimension=1,...  40.1 us
    all_to_all x1, waiting for transfers between devices, body(): gathered = lax.all_to_all(copies, 'head', 1, 1, tiled=True)  38.3 us
    all_gather x2, waiting for transfers between devices, entering(): lax.all_gather(part.astype(kind), axis)  32.1 us
    unnamed x1, blocking collectives  15.7 us
    dot_general x1, matrix products, body(): proj_sum = jnp.dot(source, pieces[0], preferred_element_type=jnp.float32)  14.2 us
    dot_general x3, matrix products, advance(): within = jnp.einsum('ijh,jhp->ihp', weights, stretch_in, precision=HIGHEST)  9.8 us
  transfers between devices with their start and end apart: 6, of which 6 were waited for; matrix products, arithmetic and copies ran while one was open for 5% of the time, Pallas kernels for 0%

profile of v1, /device:TPU:8, one launch (start us, length us, event | category | flops | bytes accessed | tf_op | source)
XLA Modules:
  0.0 387.9 jit_solution(8331059611487835285)
XLA Ops:
  10.1 3.0 copy.105
  13.1 4.6 %all-to-all-start = ((bf16[384,8,512]{2,0,1:T(8,128)(2,1)}), bf16[384,8,512]{2,0,1:T(8,128)(2,1)}, u32[]{:S(2)}, u32[]{:S(2)}) async-start(bf16[384,8,512]{2,0,1:T(8,128)(2,1)} %copy.105), calls=%async_computation | async-start | bytes 6291456 | tf_op jit(solution)/shard_map/all_to_all | solution.py:114
  17.7 38.3 %all-to-all-done = bf16[384,8,512]{2,0,1:T(8,128)(2,1)} async-done(((bf16[384,8,512]{2,0,1:T(8,128)(2,1)}), bf16[384,8,512]{2,0,1:T(8,128)(2,1)}, u32[]{:S(2)}, u32[]{:S(2)}) %all-to-all-start) | async-done | bytes 3145760 | tf_op jit(solution)/shard_map/all_to_all | solution.py:114
  56.1 3.5 copy.106
  64.4 4.0 %collective-permute-start = (bf16[3,4096]{1,0:T(4,128)(2,1)S(1)}, bf16[3,4096]{1,0:T(4,128)(2,1)S(1)}, u32[]{:S(2)}, u32[]{:S(2)}) collective-permute-start(bf16[3,4096]{1,0:T(4,128)(2,1)S(1)} %copy.107), channel_id=1, source_target_pairs={{0,8},{8,16},{16,24},{24,32},{32,40},{40,48},{48,56},{56,64},{64,7... | collective-permute-start | bytes 73736 | tf_op jit(solution)/shard_map/ppermute | solution.py:17
  68.6 6.1 %collective-permute-done = bf16[3,4096]{1,0:T(4,128)(2,1)S(1)} collective-permute-done((bf16[3,4096]{1,0:T(4,128)(2,1)S(1)}, bf16[3,4096]{1,0:T(4,128)(2,1)S(1)}, u32[]{:S(2)}, u32[]{:S(2)}) %collective-permute-start) | collective-permute-done | bytes 24608 | tf_op jit(solution)/shard_map/ppermute | solution.py:17
  75.2 91.9 %all-gather.6.cloned.1.call-done = bf16[4096,2320]{1,0:T(8,128)(2,1)} async-done(((bf16[128,2320]{1,0:T(8,128)(2,1)}), bf16[4096,2320]{1,0:T(8,128)(2,1)}) %all-gather.6.cloned.1.call-update) | async-done | bytes 19005456 | tf_op jit(solution)/shard_map/all_gather | solution.py:22
  167.1 14.2 %fusion.56 = bf16[387,1,2304]{2,0,1:T(8,128)(2,1)S(1)} fusion(bf16[4096,2320]{1,0:T(8,128)(2,1)} %all-gather.6.cloned.1.call-done, bf16[384,4096]{0,1:T(8,128)(2,1)} %fusion.46, bf16[3,4096]{0,1:T(8,128)(2,1)S(1)} %copy.108), kind=kOutput, calls=%fused_computation.63 | convolution fusion | flops 7311612928 | bytes 23827968 | tf_op jit(solution)/shard_map/dot_general | solution.py:121
  183.4 3.1 fusion.163
  190.2 3.2 copy.113
  193.4 64.6 %while.14 = (s32[]{:T(128)}, f32[1,16,64,128]{3,2,1,0:T(8,128)S(1)}, f32[3,1,128,16,64]{2,0,4,3,1:T(4,128)}, f32[3,1,128,16]{3,2,1,0:T(8,128)}, f32[3,1,128,16]{...) while((s32[]{:T(128)}, ...), condition=%wide.region_3.4_spmd.clone.clone, body=%wide.region_1.3_spmd.clone.clone.sunk | while | flops 610682880 | bytes 5721559 | solution.py:97
  197.9 3.3 fusion.192
  201.1 13.8 %dynamic_update_slice.7 = f32[3,1,128,16,64]{2,0,4,3,1:T(4,128)} dynamic-update-slice(f32[3,1,128,16,64]{2,0,4,3,1:T(4,128)} %get-tuple-element.262, f32[1,1,128,16,64]{2,0,4,3,1:T(1,128)S(1)} %bitcast.249, s32[]{:T(128)S(6)} %copy.157, s32[]{:T(128)} %constant.25.clone.1..sunk, s32[]{:T(128)} %constant.25.clone.1..sunk, s32[]{:T(128)} %constant.25.clone.1..sunk, s32[]{:T(128)} %constant.25.clone.1..sunk) | dynamic-update-slice | bytes 1048580 | tf_op jit(solution)/shard_map/vmap()/while/body/jit(dynamic_update_index_in_dim)/dynamic_update_slice | solution.py:97
  219.4 3.3 fusion.192
  222.7 13.8 %dynamic_update_slice.7 = f32[3,1,128,16,64]{2,0,4,3,1:T(4,128)} dynamic-update-slice(f32[3,1,128,16,64]{2,0,4,3,1:T(4,128)} %get-tuple-element.262, f32[1,1,128,16,64]{2,0,4,3,1:T(1,128)S(1)} %bitcast.249, s32[]{:T(128)S(6)} %copy.157, s32[]{:T(128)} %constant.25.clone.1..sunk, s32[]{:T(128)} %constant.25.clone.1..sunk, s32[]{:T(128)} %constant.25.clone.1..sunk, s32[]{:T(128)} %constant.25.clone.1..sunk) | dynamic-update-slice | bytes 1048580 | tf_op jit(solution)/shard_map/vmap()/while/body/jit(dynamic_update_index_in_dim)/dynamic_update_slice | solution.py:97
  240.9 3.3 fusion.192
  244.2 13.8 %dynamic_update_slice.7 = f32[3,1,128,16,64]{2,0,4,3,1:T(4,128)} dynamic-update-slice(f32[3,1,128,16,64]{2,0,4,3,1:T(4,128)} %get-tuple-element.262, f32[1,1,128,16,64]{2,0,4,3,1:T(1,128)S(1)} %bitcast.249, s32[]{:T(128)S(6)} %copy.157, s32[]{:T(128)} %constant.25.clone.1..sunk, s32[]{:T(128)} %constant.25.clone.1..sunk, s32[]{:T(128)} %constant.25.clone.1..sunk, s32[]{:T(128)} %constant.25.clone.1..sunk) | dynamic-update-slice | bytes 1048580 | tf_op jit(solution)/shard_map/vmap()/while/body/jit(dynamic_update_index_in_dim)/dynamic_update_slice | solution.py:97
  260.6 15.7 %all-reduce = bf16[128]{0:T(256)(128)(2,1)S(1)} all-reduce(bf16[128]{0:T(256)(128)(2,1)S(1)} %dynamic-update-slice), channel_id=2, replica_groups=mesh['seq_0'=4,'seq_1'=8,'head'=8] {'seq_1'}, use_global_device_ids=true, to_apply=%add | all-reduce | flops 128 | bytes 512
  276.4 21.7 %all-gather.10.cloned.1.call-done = bf16[8,16,64,128]{3,2,1,0:T(8,128)(2,1)} async-done(((bf16[1,16,64,128]{3,2,1,0:T(8,128)(2,1)}), bf16[8,16,64,128]{3,2,1,0:T(8,128)(2,1)}) %all-gather.10.cloned.1.call-update) | async-done | bytes 2097168 | tf_op jit(solution)/shard_map/all_gather | solution.py:41
  301.0 7.8 %all_gather.23 = bf16[4,1,16]{2,1,0:T(2,128)(2,1)S(1)} all-gather(bf16[1,1,16]{2,1,0:T(2,128)(2,1)S(1)} %get-tuple-element.172), channel_id=1, replica_groups=mesh['seq_0'=4,'seq_1'=8,'head'=8] {'seq_0'}, dimensions={0}, use_global_device_ids=true | all-gather | bytes 160 | tf_op jit(solution)/shard_map/all_gather | solution.py:41
  314.7 10.3 %all-gather.8.cloned.1.call-done = bf16[4,1,16,64,128]{4,3,2,1,0:T(8,128)(2,1)} async-done(((bf16[1,1,16,64,128]{4,3,2,1,0:T(8,128)(2,1)}), bf16[4,1,16,64,128]{4,3,2,1,0:T(8,128)(2,1)}) %all-gather.8.cloned.1.call-update) | async-done | bytes 1048592 | tf_op jit(solution)/shard_map/all_gather | solution.py:41
  325.0 4.7 %fusion.70 = f32[384,1,16,64]{0,3,2,1:T(8,128)} fusion(f32[384,1,16,64]{0,3,2,1:T(8,128)S(1)} %transpose.64, f32[384,1,16,64]{0,3,2,1:T(8,128)S(1)} %bitcast.253, f32[16]{0:T(128)S(1)} %copy-done.11, f32[384,16]{0,1:T(8,128)S(1)} %fusion.140, bf16[4,1,16,64,128]{4,3,2,1,0:T(8,128)(2,1)} %all-gather.8.cloned.1.call-done, f32[16]{0:T(128)S(1)} %get-tuple-element.189, ...), kind=kOutput, calls=%fused_computation.77 | convolution fusion | flops 611844096 | bytes 7988108 | tf_op jit(solution)/shard_map/tgn,ghpn->tghp/dot_general | solution.py:148
  332.4 8.8 %fusion.47 = bf16[384,4096]{1,0:T(8,128)(2,1)} fusion(bf16[1,1024,4096]{2,1,0:T(8,128)(2,1)} %param.23, f32[1024]{0:T(1024)S(1)} %bitcast.257, f32[384]{0:T(512)S(1)} %add_rsqrt_fusion, f32[384,1,1024]{2,0,1:T(8,128)S(1)} %copy.121, bf16[387,1,2304]{2,0,1:T(8,128)(2,1)S(1)} %copy-done.1), kind=kOutput, calls=%fused_computation.58 | convolution fusion | flops 3226337280 | bytes 13899776 | tf_op jit(solution)/shard_map/dot_general | solution.py:157
  341.2 40.1 %reduce-scatter.2.cloned.1.call-done = bf16[384,512]{1,0:T(8,128)(2,1)} async-done(((bf16[384,4096]{1,0:T(8,128)(2,1)}), bf16[384,512]{1,0:T(8,128)(2,1)}) %reduce-scatter.2.cloned.1.call-update) | async-done | bytes 393232 | tf_op jit(solution)/shard_map/reduce_scatter | solution.py:162
  (124 shorter events, 41.3 us)
Async XLA Ops:
  6.5 2.8 copy-start.4
  6.5 160.6 %all-gather.6.cloned.1.call-start = ((), (), s32[]{:S(2)}) async-start(), calls=%async_computation.2 | async-start | bytes 20545536 | tf_op jit(solution)/shard_map/all_gather | solution.py:22
  13.1 4.6 %copy-start.9 = (f32[16]{0:T(128)S(1)}, f32[16]{0:T(128)}, u32[]{:S(2)}) copy-start(f32[16]{0:T(128)} %param.18) | copy-start | bytes 196
  13.1 43.0 %all-to-all-start = ((bf16[384,8,512]{2,0,1:T(8,128)(2,1)}), bf16[384,8,512]{2,0,1:T(8,128)(2,1)}, u32[]{:S(2)}, u32[]{:S(2)}) async-start(bf16[384,8,512]{2,0,1:T(8,128)(2,1)} %copy.105), calls=%async_computation | async-start | bytes 6291456 | tf_op jit(solution)/shard_map/all_to_all | solution.py:114
  17.7 280.5 %all-gather.10.cloned.1.call-start = ((), (), s32[]{:S(2)}) async-start(), calls=%async_computation.5 | async-start | bytes 2359296 | tf_op jit(solution)/shard_map/all_gather | solution.py:41
  59.5 0.8 copy-start.6
  62.4 6.0 %copy-start.5 = (f32[4,1,1280]{2,1,0:T(1,128)S(1)}, f32[4,1,1280]{2,1,0:T(1,128)}, u32[]{:S(2)}) copy-start(f32[4,1,1280]{2,1,0:T(1,128)} %param.20) | copy-start | bytes 61444
  62.5 6.1 %copy-start.7 = (f32[1,1280]{1,0:T(1,128)S(1)}, f32[1,1280]{1,0:T(1,128)}, u32[]{:S(2)}) copy-start(f32[1,1280]{1,0:T(1,128)} %param.21) | copy-start | bytes 15364
  64.4 10.2 %collective-permute-start = (bf16[3,4096]{1,0:T(4,128)(2,1)S(1)}, bf16[3,4096]{1,0:T(4,128)(2,1)S(1)}, u32[]{:S(2)}, u32[]{:S(2)}) collective-permute-start(bf16[3,4096]{1,0:T(4,128)(2,1)S(1)} %copy.107), channel_id=1, source_target_pairs={{0,8},{8,16},{16,24},{24,32},{32,40},{40,48},{48,56},{56,64},{64,7... | collective-permute-start | bytes 73736 | tf_op jit(solution)/shard_map/ppermute | solution.py:17
  181.3 1.3 copy-start
  182.7 3.8 copy-start.2
  182.7 0.7 copy-start.10
  193.4 65.7 %copy-start.12 = (u32[256]{0:T(256)S(1)}, u32[256]{0:T(256)}, u32[]{:S(2)}) copy-start(u32[256]{0:T(256)} %constant.77) | copy-start | bytes 3076
  258.8 66.2 %all-gather.8.cloned.1.call-start = ((), (), s32[]{:S(2)}) async-start(), calls=%async_computation.3 | async-start | bytes 1310720 | tf_op jit(solution)/shard_map/all_gather | solution.py:41
  301.0 80.4 %reduce-scatter.2.cloned.1.call-start = ((), (), s32[]{:S(2)}) async-start(), calls=%async_computation.4 | async-start | bytes 3538944 | tf_op jit(solution)/shard_map/reduce_scatter | solution.py:162
  310.5 14.6 %copy-start.3 = (f32[384,1,1024]{0,2,1:T(8,128)S(1)}, f32[384,1,1024]{0,2,1:T(8,128)}, u32[]{:S(2)}) copy-start(f32[384,1,1024]{0,2,1:T(8,128)} %copy.120) | copy-start | bytes 4718596
  310.5 14.6 %copy-start.11 = (f32[16]{0:T(128)S(1)}, f32[16]{0:T(128)}, u32[]{:S(2)}) copy-start(f32[16]{0:T(128)} %param.19) | copy-start | bytes 196
  329.7 2.0 copy-start.1
  329.7 2.7 copy-start.8
Sparse Core Ops, SparseCore 0:
  9.9 157.1 all-gather.5
  258.9 39.2 all-gather.9
  301.1 23.8 all-gather.7
  341.4 39.9 reduce-scatter.1
